TPU v7x, 512 devices: a whole 4x4x16 slice. The times are simulated.
512 devices in a mesh: frow: 32 (over z_lo, y, core), fcol: 16 (over z_hi, x).
Axes of the slice: x: 4, y: 4, z: 16 (z_hi: 4, z_lo: 4; z = z_hi * 4 + z_lo), core: 2. Of those that a mesh axis runs over, the one named last changes fastest.
Arguments:
- model_image: bfloat16 [16384, 16384], P('frow', 'fcol'), may hold values from -6 to 6
- weight_grids: bfloat16 [8, 256, 256], replicated, may hold values from 0.19921875 to 2
- strip_offsets: int32 [2], replicated, may hold values from 0 to 63
- subgrid_offsets: int32 [2, 32], replicated, may hold values from 0 to 63
- grid_index: int32 [2, 32], replicated, may hold values from 0 to 7
Outputs:
- residual_update: float32 [16384, 16384], P('frow', 'fcol')
Inputs may be any that keep to these rules, and one draw needn't show every extreme that they name: `strip_offsets`: two strips may coincide. `subgrid_offsets`: two subgrids of one strip may coincide.
All inputs are finite; a program needn't handle non-finite values.
Results may differ from a plain program's by a relative error of at most 0.03.
Values may be sent and summed in bfloat16 or wider, within the bound.
No kernel may reach another device: no remote copies, remote signals or barrier semaphores. Data moves between devices by JAX's collectives and lax.ppermute only.
A program may use at most 64 MiB of HBM per device.

v0:
```python
import math
import jax
import jax.numpy as jnp
from jax import lax
from jax.sharding import PartitionSpec as P

STRIP = 256


def split_up(value, dim, length):
    dims = value.shape
    parts = value.reshape(*dims[:dim], length, dims[dim] // length, *dims[dim + 1 :])
    return jnp.moveaxis(parts, dim, 0)


def sent_and_summed(value, axis, dim):
    length = lax.axis_size(axis)
    parts = lax.all_to_all(split_up(value, dim, length), axis, 0, 0, tiled=True)
    return jnp.sum(parts.astype(jnp.float32), axis=0)


def joined_along(parts, dim):
    parts = jnp.moveaxis(parts, 0, dim)
    dims = parts.shape
    return parts.reshape(*dims[:dim], dims[dim] * dims[dim + 1], *dims[dim + 2 :])


def copy_for_each(value, axis):
    copies = jnp.broadcast_to(value, (lax.axis_size(axis), *value.shape))
    return lax.all_to_all(copies, axis, split_axis=0, concat_axis=0, tiled=True)


def gathered_copies(value, axis, dim):
    return joined_along(copy_for_each(value, axis), dim)


def phase_pair(leading, trailing, modulus, factor):
    turns = leading[:, None] * trailing[None, :] % modulus
    angle = turns.astype(jnp.float32) * (2.0 * math.pi / modulus)
    return (jnp.cos(angle) * factor, jnp.sin(angle) * factor)


def modulate(strip_real, strip_imag, cos_shift, sin_shift):
    real_part = strip_real[None] * cos_shift[:, None, :] + strip_imag[None] * sin_shift[:, None, :]
    imag_part = strip_imag[None] * cos_shift[:, None, :] - strip_real[None] * sin_shift[:, None, :]
    return jnp.concatenate([real_part, imag_part], axis=2).astype(jnp.bfloat16)


def demodulate(spectra, cos_shift, sin_shift, width):
    real_in = spectra[:, :, :width]
    imag_in = spectra[:, :, width:]
    real_part = jnp.sum(real_in * cos_shift[:, None, :] - imag_in * sin_shift[:, None, :], axis=0)
    imag_part = jnp.sum(imag_in * cos_shift[:, None, :] + real_in * sin_shift[:, None, :], axis=0)
    return jnp.concatenate([real_part, imag_part], axis=1)


def forward_table(pixels, sub_width, modulus, factor):
    spaced = jnp.arange(sub_width, dtype=jnp.int32) * (modulus // sub_width)
    cosine, sine = phase_pair(pixels, spaced, modulus, factor)
    upper = jnp.concatenate([cosine, -sine], axis=1)
    lower = jnp.concatenate([sine, cosine], axis=1)
    return jnp.concatenate([upper, lower], axis=0).astype(jnp.bfloat16)


def backward_table(pixels, sub_width, modulus, factor):
    spaced = jnp.arange(sub_width, dtype=jnp.int32) * (modulus // sub_width)
    cosine, sine = phase_pair(spaced, pixels, modulus, factor)
    upper = jnp.concatenate([cosine, sine], axis=1)
    lower = jnp.concatenate([-sine, cosine], axis=1)
    return jnp.concatenate([upper, lower], axis=0).astype(jnp.bfloat16)


def body(model_image, weight_grids, strip_offsets, subgrid_offsets, grid_index):
    rows_local, facet_width = model_image.shape
    row_groups = lax.axis_size("frow")
    modulus = facet_width * lax.axis_size("fcol")
    uv_rows = strip_offsets.shape[0] * STRIP
    share_rows = uv_rows // row_groups
    sub_width = weight_grids.shape[2]
    subgrid_count = subgrid_offsets.shape[1]
    forward_scale = 1.0 / math.sqrt(modulus)
    column_scale = 1.0 / math.sqrt(subgrid_count * sub_width)
    row_scale = 1.0 / math.sqrt(uv_rows)
    row_index = lax.axis_index("frow")
    pixel_rows = row_index * rows_local + jnp.arange(rows_local, dtype=jnp.int32)
    pixel_cols = lax.axis_index("fcol") * facet_width + jnp.arange(facet_width, dtype=jnp.int32)
    row_spacing = modulus // STRIP
    frequencies = (
        strip_offsets[:, None] + jnp.arange(STRIP, dtype=jnp.int32)[None, :] * row_spacing
    ).reshape(uv_rows)
    wanted = frequencies
    cosine, sine = phase_pair(wanted, pixel_rows, modulus, forward_scale)
    phases = jnp.concatenate([cosine, sine], axis=0).astype(jnp.bfloat16)
    stacked = jnp.dot(phases, model_image, preferred_element_type=jnp.float32)
    mine = sent_and_summed(
        jnp.concatenate(
            [
                stacked[: share_rows * lax.axis_size("frow")],
                -stacked[share_rows * lax.axis_size("frow") :],
            ],
            axis=1,
        ).astype(jnp.bfloat16),
        "frow",
        0,
    )
    strip = mine.astype(jnp.bfloat16)
    strip_real = strip[:, :facet_width]
    strip_imag = strip[:, facet_width:]
    first_global = row_index * share_rows
    strip_number = first_global // STRIP
    strip_row = first_global % STRIP
    my_shifts = lax.dynamic_index_in_dim(subgrid_offsets, strip_number, 0, keepdims=False)
    my_grids = lax.dynamic_index_in_dim(grid_index, strip_number, 0, keepdims=False)
    my_table = lax.dynamic_slice_in_dim(weight_grids, strip_row, share_rows, 1)
    ahead = forward_table(pixel_cols, sub_width, modulus, forward_scale)
    behind = backward_table(pixel_cols, sub_width, modulus, column_scale)
    local_count = subgrid_count // lax.axis_size("fcol")
    shifts = my_shifts
    cos_shift, sin_shift = phase_pair(shifts, pixel_cols, modulus, 1.0)
    modulated = modulate(strip_real, strip_imag, cos_shift, sin_shift)
    flat = modulated.reshape(local_count * lax.axis_size("fcol") * share_rows, 2 * facet_width)
    spectra = jnp.dot(flat, ahead, preferred_element_type=jnp.float32)
    owned = sent_and_summed(
        spectra.reshape(local_count * lax.axis_size("fcol"), share_rows, 2 * sub_width).astype(
            jnp.bfloat16
        ),
        "fcol",
        0,
    )
    chosen = lax.dynamic_slice_in_dim(
        my_grids, lax.axis_index("fcol") * local_count, owned.shape[0]
    )
    grids = jnp.take(my_table, chosen, axis=0).astype(jnp.float32)
    owned_weighted = (owned * jnp.concatenate([grids, grids], axis=2)).astype(jnp.bfloat16)
    shards = gathered_copies(owned_weighted, "fcol", 0)
    shifts = my_shifts
    cos_shift, sin_shift = phase_pair(shifts, pixel_cols, modulus, 1.0)
    flat = shards.reshape(shards.shape[0] * share_rows, 2 * sub_width)
    spectra = jnp.dot(flat, behind, preferred_element_type=jnp.float32)
    spectra = spectra.reshape(shards.shape[0], share_rows, 2 * facet_width)
    merged = demodulate(spectra, cos_shift, sin_shift, facet_width)
    strip_image = merged.astype(jnp.bfloat16)
    shards = lax.all_gather(strip_image, "frow", axis=0, tiled=True)
    wanted = frequencies
    cosine, sine = phase_pair(pixel_rows, wanted, modulus, row_scale)
    phases = jnp.concatenate([cosine, -sine], axis=1).astype(jnp.bfloat16)
    stacked = jnp.concatenate([shards[:, :facet_width], shards[:, facet_width:]], axis=0)
    return jnp.dot(phases, stacked, preferred_element_type=jnp.float32)


def solution(mesh):
    return jax.shard_map(
        body,
        mesh=mesh,
        in_specs=(P("frow", "fcol"), P(), P(), P(), P()),
        out_specs=P("frow", "fcol"),
        check_vma=False,
    )
```

profile of v0, /device:TPU:1, one launch (start us, length us, event | category | flops | bytes accessed | tf_op | source)
XLA Modules:
  0.0 238.4 jit_solution(12703936831153355637)
XLA Ops:
  6.5 0.0 copy-start
  6.5 0.8 add_bitcast_fusion
  7.4 9.9 %multiply_convert_fusion.4 = (bf16[512,512]{1,0:T(8,128)(2,1)}, bf16[512,512]{1,0:T(8,128)(2,1)}, bf16[512,512]{1,0:T(8,128)(2,1)S(1)}, bf16[512,512]{1,0:T(8,128)(2,1)S(1)}) fusion(s32[512]{0:T(512)S(1)} %bitcast.28, s32[512]{0:T(512)S(1)} %iota_add_fusion.1), kind=kLoop, calls=%fused_computation.82 | loop fusion | flops 9699328 | bytes 2101248 | tf_op jit(solution)/shard_map/convert.25
  17.2 0.0 copy-done
  17.2 1.3 fusion.40
  18.5 0.2 slice.53
  18.7 0.3 fusion
  18.9 1.5 pad_maximum_fusion
  20.4 0.0 copy-start.7
  20.4 10.6 %all-to-all-start = ((bf16[32,16,2048]{2,1,0:T(8,128)(2,1)}), bf16[32,16,2048]{2,1,0:T(8,128)(2,1)S(1)}, u32[]{:S(2)}, u32[]{:S(2)}) async-start(bf16[32,16,2048]{2,1,0:T(8,128)(2,1)} %pad_maximum_fusion), calls=%async_computation | async-start | bytes 4194304 | tf_op jit(solution)/shard_map/all_to_all | solution.py:18
  31.1 0.0 copy-done.7
  31.1 0.6 fusion.50
  31.7 5.8 %negate_convert_fusion.1 = (bf16[1024,256]{1,0:T(8,128)(2,1)}, bf16[1024,256]{1,0:T(8,128)(2,1)}, bf16[1024,256]{1,0:T(8,128)(2,1)}) fusion(s32[256]{0:T(256)S(1)} %iota_multiply_fusion, s32[1024]{0:T(1024)S(1)} %iota_add_fusion), kind=kLoop, calls=%fused_computation.76 | loop fusion | flops 5242880 | bytes 1577984 | tf_op jit(solution)/shard_map/convert.15
  37.6 41.6 %all-to-all-done = bf16[32,16,2048]{2,1,0:T(8,128)(2,1)S(1)} async-done(((bf16[32,16,2048]{2,1,0:T(8,128)(2,1)}), bf16[32,16,2048]{2,1,0:T(8,128)(2,1)S(1)}, u32[]{:S(2)}, u32[]{:S(2)}) %all-to-all-start) | async-done | bytes 2097184 | tf_op jit(solution)/shard_map/all_to_all | solution.py:18
  79.2 0.3 reduce_sum.39
  79.5 0.0 copy-start.3
  79.5 0.0 copy-start.4
  79.5 0.0 copy-start.5
  79.5 0.7 add_convert_fusion
  80.3 0.3 copy-done.3
  80.5 0.2 copy-done.4
  80.7 0.2 copy-done.5
  80.9 2.0 fusion.22
  82.9 14.2 %all-to-all-start.1 = ((bf16[16,2,16,512]{3,2,1,0:T(8,128)(2,1)}), bf16[16,2,16,512]{3,2,1,0:T(8,128)(2,1)S(1)}, u32[]{:S(2)}, u32[]{:S(2)}) async-start(bf16[16,2,16,512]{3,2,1,0:T(8,128)(2,1)} %bitcast.4), calls=%async_computation.1 | async-start | bytes 1048576 | tf_op jit(solution)/shard_map/all_to_all | solution.py:18
  97.2 0.0 copy-done.6
  97.2 0.1 fusion.51
  97.3 0.8 constant_dynamic-slice_fusion
  98.1 0.5 gather_fusion
  98.7 0.1 compare_and_fusion
  98.8 0.1 broadcast_select_fusion
  98.8 16.1 %all-to-all-done.1 = bf16[16,2,16,512]{3,2,1,0:T(8,128)(2,1)S(1)} async-done(((bf16[16,2,16,512]{3,2,1,0:T(8,128)(2,1)}), bf16[16,2,16,512]{3,2,1,0:T(8,128)(2,1)S(1)}, u32[]{:S(2)}, u32[]{:S(2)}) %all-to-all-start.1) | async-done | bytes 524320 | tf_op jit(solution)/shard_map/all_to_all | solution.py:18
  114.9 0.1 convert_reduce_fusion
  115.0 0.9 broadcast_in_dim.11
  115.9 19.8 %all-to-all-start.2 = ((bf16[16,2,16,512]{3,2,1,0:T(8,128)(2,1)}), bf16[16,2,16,512]{3,2,1,0:T(8,128)(2,1)S(1)}, u32[]{:S(2)}, u32[]{:S(2)}) async-start(bf16[16,2,16,512]{3,2,1,0:T(8,128)(2,1)} %broadcast_in_dim.11), calls=%async_computation.2 | async-start | bytes 1048576 | tf_op jit(solution)/shard_map/all_to_all | solution.py:30
  135.7 0.0 all-gather.2.cloned.1.call-start
  135.8 4.6 %fusion.45 = (bf16[256,1024]{1,0:T(8,128)(2,1)S(1)}, bf16[256,1024]{1,0:T(8,128)(2,1)S(1)}, bf16[256,1024]{1,0:T(8,128)(2,1)S(1)}) fusion(s32[1024]{0:T(1024)S(1)} %iota_add_fusion, s32[256]{0:T(256)S(1)} %iota_multiply_fusion), kind=kLoop, calls=%fused_computation.84 | loop fusion | flops 5242880 | bytes 1577984 | tf_op jit(solution)/shard_map/convert.9
  140.4 24.2 %all-to-all-done.2 = bf16[16,2,16,512]{3,2,1,0:T(8,128)(2,1)S(1)} async-done(((bf16[16,2,16,512]{3,2,1,0:T(8,128)(2,1)}), bf16[16,2,16,512]{3,2,1,0:T(8,128)(2,1)S(1)}, u32[]{:S(2)}, u32[]{:S(2)}) %all-to-all-start.2) | async-done | bytes 524320 | tf_op jit(solution)/shard_map/all_to_all | solution.py:30
  164.6 1.3 fusion.11
  165.8 0.7 subtract_reduce_fusion
  166.5 0.6 pad_maximum_fusion.1
  167.1 0.0 all-gather.2.cloned.1.call-update
  167.2 0.0 copy-start.1
  167.2 0.0 copy-start.2
  167.2 60.1 %all-gather.2.cloned.1.call-done = bf16[512,2048]{1,0:T(8,128)(2,1)} async-done(((bf16[16,2048]{1,0:T(8,128)(2,1)}), bf16[512,2048]{1,0:T(8,128)(2,1)}) %all-gather.2.cloned.1.call-update) | async-done | bytes 2097168 | tf_op jit(solution)/shard_map/all_gather | solution.py:143
  227.2 1.7 fusion.56
  228.9 0.0 copy-done.1
  229.0 0.0 copy-done.2
  229.0 2.6 %fusion.18 = f32[512,1024]{1,0:T(8,128)} fusion(bf16[512,1024]{1,0:T(8,128)(2,1)S(1)} %get-tuple-element.8, bf16[512,1024]{1,0:T(8,128)(2,1)S(1)} %get-tuple-element.7, bf16[512,512]{1,0:T(8,128)(2,1)S(1)} %copy-done.2, bf16[512,512]{1,0:T(8,128)(2,1)S(1)} %copy-done.1), kind=kOutput, calls=%fused_computation.24 | convolution fusion | flops 1080033280 | bytes 5242880 | tf_op jit(solution)/shard_map/dot_general | solution.py:148
  (9 shorter events, 0.1 us)
Async XLA Ops:
  6.5 10.7 %copy-start = (bf16[512,1024]{1,0:T(8,128)(2,1)S(1)}, bf16[512,1024]{1,0:T(8,128)(2,1)}, u32[]{:S(2)}) copy-start(bf16[512,1024]{1,0:T(8,128)(2,1)} %param.5) | copy-start | bytes 3145732
  20.4 10.7 %copy-start.7 = (s32[2,32]{1,0:T(2,128)S(1)}, s32[2,32]{1,0:T(2,128)}, u32[]{:S(2)}) copy-start(s32[2,32]{1,0:T(2,128)} %param.8) | copy-start | bytes 772
  20.4 58.7 %all-to-all-start = ((bf16[32,16,2048]{2,1,0:T(8,128)(2,1)}), bf16[32,16,2048]{2,1,0:T(8,128)(2,1)S(1)}, u32[]{:S(2)}, u32[]{:S(2)}) async-start(bf16[32,16,2048]{2,1,0:T(8,128)(2,1)} %pad_maximum_fusion), calls=%async_computation | async-start | bytes 4194304 | tf_op jit(solution)/shard_map/all_to_all | solution.py:18
  79.5 1.0 copy-start.3
  79.5 1.2 copy-start.4
  79.5 1.3 copy-start.5
  80.8 16.3 %copy-start.6 = (s32[2,32]{1,0:T(2,128)S(1)}, s32[2,32]{1,0:T(2,128)}, u32[]{:S(2)}) copy-start(s32[2,32]{1,0:T(2,128)} %param.9) | copy-start | bytes 772
  82.9 32.1 %all-to-all-start.1 = ((bf16[16,2,16,512]{3,2,1,0:T(8,128)(2,1)}), bf16[16,2,16,512]{3,2,1,0:T(8,128)(2,1)S(1)}, u32[]{:S(2)}, u32[]{:S(2)}) async-start(bf16[16,2,16,512]{3,2,1,0:T(8,128)(2,1)} %bitcast.4), calls=%async_computation.1 | async-start | bytes 1048576 | tf_op jit(solution)/shard_map/all_to_all | solution.py:18
  115.9 48.7 %all-to-all-start.2 = ((bf16[16,2,16,512]{3,2,1,0:T(8,128)(2,1)}), bf16[16,2,16,512]{3,2,1,0:T(8,128)(2,1)S(1)}, u32[]{:S(2)}, u32[]{:S(2)}) async-start(bf16[16,2,16,512]{3,2,1,0:T(8,128)(2,1)} %broadcast_in_dim.11), calls=%async_computation.2 | async-start | bytes 1048576 | tf_op jit(solution)/shard_map/all_to_all | solution.py:30
  135.7 91.5 %all-gather.2.cloned.1.call-start = ((), (), s32[]{:S(2)}) async-start(), calls=%async_computation.3 | async-start | bytes 2162688 | tf_op jit(solution)/shard_map/all_gather | solution.py:143
  167.2 61.8 %copy-start.1 = (bf16[512,512]{1,0:T(8,128)(2,1)S(1)}, bf16[512,512]{1,0:T(8,128)(2,1)}, u32[]{:S(2)}) copy-start(bf16[512,512]{1,0:T(8,128)(2,1)} %get-tuple-element.21) | copy-start | bytes 1572868
  167.2 61.8 %copy-start.2 = (bf16[512,512]{1,0:T(8,128)(2,1)S(1)}, bf16[512,512]{1,0:T(8,128)(2,1)}, u32[]{:S(2)}) copy-start(bf16[512,512]{1,0:T(8,128)(2,1)} %get-tuple-element.22) | copy-start | bytes 1572868
Sparse Core Ops, SparseCore 0:
  167.3 59.9 all-gather.1
where the time goes:
time: 239 us; the launch traced here: 238 us
  waiting for transfers between devices  142 us (59%)
  starting transfers between devices  44.7 us (19%)
  other arithmetic  26.2 us (11%)
  between operations  13.6 us (6%)
  matrix products  7.13 us (3%)
  local copies, waits for them, and re-layouts  4.74 us (2%)
    all_gather x1, waiting for transfers between devices, body(): shards = lax.all_gather(strip_image, 'frow', axis=0, tiled=True)  60.1 us
    all_to_all x2, waiting for transfers between devices, sent_and_summed(): parts = lax.all_to_all(split_up(value, dim, length), axis, 0, 0, tiled=True)  57.7 us
    all_to_all x2, starting transfers between devices, sent_and_summed(): parts = lax.all_to_all(split_up(value, dim, length), axis, 0, 0, tiled=True)  24.9 us
    all_to_all x1, waiting for transfers between devices, copy_for_each(): return lax.all_to_all(copies, axis, split_axis=0, concat_axis=0, tiled=True)  24.2 us
    another operation x5, other arithmetic  21.3 us
    all_to_all x1, starting transfers between devices, copy_for_each(): return lax.all_to_all(copies, axis, split_axis=0, concat_axis=0, tiled=True)  19.8 us
  transfers between devices with their start and end apart: 4, of which 4 were waited for; matrix products, arithmetic and copies ran while one was open for 5% of the time, Pallas kernels for 0%

commit v1 on v0

--- a/solution.py
+++ b/solution.py
@@ -140,7 +140,9 @@
     spectra = spectra.reshape(shards.shape[0], share_rows, 2 * facet_width)
     merged = demodulate(spectra, cos_shift, sin_shift, facet_width)
     strip_image = merged.astype(jnp.bfloat16)
-    shards = lax.all_gather(strip_image, "frow", axis=0, tiled=True)
+    shards = jnp.concatenate(
+        lax.all_to_all(jnp.stack([strip_image] * lax.axis_size("frow"), 0), "frow", 0, 0), axis=0
+    )
     wanted = frequencies
     cosine, sine = phase_pair(pixel_rows, wanted, modulus, row_scale)
     phases = jnp.concatenate([cosine, -sine], axis=1).astype(jnp.bfloat16)

time: 239 us -> 222 us (0.929)
  waiting for transfers between devices: 142 us -> 81.9 us
  blocking collectives: 0 us -> 57.2 us
  between operations: 13.6 us -> 0.24 us
    all_gather x1 -> x0, waiting for transfers between devices: 60.1 us -> none  [body(): shards = lax.all_gather(strip_image, 'frow', axis=0, tiled=True)]
    all_to_all x0 -> x1, blocking collectives: none -> 57.2 us  [body(): lax.all_to_all(jnp.stack([strip_image] * lax.axis_size('frow'), 0), 'frow...]
  transfers between devices with their start and end apart: 4 -> 3, of which waited for: 4 -> 3; matrix products, arithmetic and copies ran while one was open for 5% -> 6% of each run, Pallas kernels for 0% -> 0%
where the time goes in v1:
time: 222 us; the launch traced here: 221 us
  waiting for transfers between devices  81.9 us (37%)
  blocking collectives  57.2 us (26%)
  starting transfers between devices  44.7 us (20%)
  other arithmetic  25.6 us (12%)
  matrix products  7.12 us (3%)
  local copies, waits for them, and re-layouts  4.45 us (2%)
    all_to_all x2, waiting for transfers between devices, sent_and_summed(): parts = lax.all_to_all(split_up(value, dim, length), axis, 0, 0, tiled=True)  57.6 us
    all_to_all x1, blocking collectives, body(): lax.all_to_all(jnp.stack([strip_image] * lax.axis_size('frow'), 0), 'frow...  57.2 us
    all_to_all x2, starting transfers between devices, sent_and_summed(): parts = lax.all_to_all(split_up(value, dim, length), axis, 0, 0, tiled=True)  24.9 us
    all_to_all x1, waiting for transfers between devices, copy_for_each(): return lax.all_to_all(copies, axis, split_axis=0, concat_axis=0, tiled=True)  24.3 us
    another operation x5, other arithmetic  21.3 us
    all_to_all x1, starting transfers between devices, copy_for_each(): return lax.all_to_all(copies, axis, split_axis=0, concat_axis=0, tiled=True)  19.8 us
  transfers between devices with their start and end apart: 3, of which 3 were waited for; matrix products, arithmetic and copies ran while one was open for 6% of the time, Pallas kernels for 0%

profile of v1, /device:TPU:1, one launch (start us, length us, event | category | flops | bytes accessed | tf_op | source)
XLA Modules:
  0.0 221.2 jit_solution(4029756052198464532)
XLA Ops:
  0.0 0.0 copy-start
  0.0 0.8 add_bitcast_fusion
  0.8 9.9 %multiply_convert_fusion.4 = (bf16[512,512]{1,0:T(8,128)(2,1)}, bf16[512,512]{1,0:T(8,128)(2,1)}, bf16[512,512]{1,0:T(8,128)(2,1)S(1)}, bf16[512,512]{1,0:T(8,128)(2,1)S(1)}) fusion(s32[512]{0:T(512)S(1)} %bitcast.30, s32[512]{0:T(512)S(1)} %iota_add_fusion.1), kind=kLoop, calls=%fused_computation.82 | loop fusion | flops 9699328 | bytes 2101248 | tf_op jit(solution)/shard_map/convert.25
  10.7 0.0 copy-done
  10.7 1.3 fusion.40
  12.0 0.2 slice.53
  12.1 0.3 fusion
  12.4 1.5 pad_maximum_fusion
  13.9 0.0 copy-start.7
  13.9 10.6 %all-to-all-start = ((bf16[32,16,2048]{2,1,0:T(8,128)(2,1)}), bf16[32,16,2048]{2,1,0:T(8,128)(2,1)S(1)}, u32[]{:S(2)}, u32[]{:S(2)}) async-start(bf16[32,16,2048]{2,1,0:T(8,128)(2,1)} %pad_maximum_fusion), calls=%async_computation | async-start | bytes 4194304 | tf_op jit(solution)/shard_map/all_to_all | solution.py:18
  24.6 0.0 copy-done.7
  24.6 0.6 fusion.50
  25.2 5.9 %negate_convert_fusion.1 = (bf16[1024,256]{1,0:T(8,128)(2,1)}, bf16[1024,256]{1,0:T(8,128)(2,1)}, bf16[1024,256]{1,0:T(8,128)(2,1)}) fusion(s32[256]{0:T(256)S(1)} %iota_multiply_fusion, s32[1024]{0:T(1024)S(1)} %iota_add_fusion), kind=kLoop, calls=%fused_computation.76 | loop fusion | flops 5242880 | bytes 1577984 | tf_op jit(solution)/shard_map/convert.15
  31.1 41.5 %all-to-all-done = bf16[32,16,2048]{2,1,0:T(8,128)(2,1)S(1)} async-done(((bf16[32,16,2048]{2,1,0:T(8,128)(2,1)}), bf16[32,16,2048]{2,1,0:T(8,128)(2,1)S(1)}, u32[]{:S(2)}, u32[]{:S(2)}) %all-to-all-start) | async-done | bytes 2097184 | tf_op jit(solution)/shard_map/all_to_all | solution.py:18
  72.6 0.3 reduce_sum.39
  72.9 0.0 copy-start.3
  73.0 0.0 copy-start.4
  73.0 0.0 copy-start.5
  73.0 0.7 add_convert_fusion
  73.7 0.3 copy-done.3
  74.0 0.2 copy-done.4
  74.1 0.2 copy-done.5
  74.3 0.0 copy-start.6
  74.3 2.0 fusion.22
  76.4 14.2 %all-to-all-start.1 = ((bf16[16,2,16,512]{3,2,1,0:T(8,128)(2,1)}), bf16[16,2,16,512]{3,2,1,0:T(8,128)(2,1)S(1)}, u32[]{:S(2)}, u32[]{:S(2)}) async-start(bf16[16,2,16,512]{3,2,1,0:T(8,128)(2,1)} %bitcast.4), calls=%async_computation.1 | async-start | bytes 1048576 | tf_op jit(solution)/shard_map/all_to_all | solution.py:18
  90.6 0.0 copy-done.6
  90.6 0.1 fusion.51
  90.7 0.8 constant_dynamic-slice_fusion
  91.6 0.5 gather_fusion
  92.1 0.1 compare_and_fusion
  92.2 0.1 broadcast_select_fusion
  92.3 16.1 %all-to-all-done.1 = bf16[16,2,16,512]{3,2,1,0:T(8,128)(2,1)S(1)} async-done(((bf16[16,2,16,512]{3,2,1,0:T(8,128)(2,1)}), bf16[16,2,16,512]{3,2,1,0:T(8,128)(2,1)S(1)}, u32[]{:S(2)}, u32[]{:S(2)}) %all-to-all-start.1) | async-done | bytes 524320 | tf_op jit(solution)/shard_map/all_to_all | solution.py:18
  108.4 0.1 convert_reduce_fusion
  108.5 0.9 broadcast_in_dim.11
  109.4 19.8 %all-to-all-start.2 = ((bf16[16,2,16,512]{3,2,1,0:T(8,128)(2,1)}), bf16[16,2,16,512]{3,2,1,0:T(8,128)(2,1)S(1)}, u32[]{:S(2)}, u32[]{:S(2)}) async-start(bf16[16,2,16,512]{3,2,1,0:T(8,128)(2,1)} %broadcast_in_dim.11), calls=%async_computation.2 | async-start | bytes 1048576 | tf_op jit(solution)/shard_map/all_to_all | solution.py:30
  129.2 4.6 %fusion.45 = (bf16[256,1024]{1,0:T(8,128)(2,1)S(1)}, bf16[256,1024]{1,0:T(8,128)(2,1)S(1)}, bf16[256,1024]{1,0:T(8,128)(2,1)S(1)}) fusion(s32[1024]{0:T(1024)S(1)} %iota_add_fusion, s32[256]{0:T(256)S(1)} %iota_multiply_fusion), kind=kLoop, calls=%fused_computation.84 | loop fusion | flops 5242880 | bytes 1577984 | tf_op jit(solution)/shard_map/convert.9
  133.8 24.3 %all-to-all-done.2 = bf16[16,2,16,512]{3,2,1,0:T(8,128)(2,1)S(1)} async-done(((bf16[16,2,16,512]{3,2,1,0:T(8,128)(2,1)}), bf16[16,2,16,512]{3,2,1,0:T(8,128)(2,1)S(1)}, u32[]{:S(2)}, u32[]{:S(2)}) %all-to-all-start.2) | async-done | bytes 524320 | tf_op jit(solution)/shard_map/all_to_all | solution.py:30
  158.0 1.3 fusion.11
  159.3 0.7 subtract_reduce_fusion
  160.0 0.2 stack.2
  160.2 57.2 %all_to_all.20 = bf16[32,16,2048]{2,1,0:T(8,128)(2,1)S(1)} all-to-all(bf16[32,16,2048]{2,1,0:T(8,128)(2,1)S(1)} %stack.2), channel_id=1, replica_groups=mesh['frow'=32,'fcol'=16] {'frow'}, dimensions={0} | all-to-all | bytes 4194304 | tf_op jit(solution)/shard_map/all_to_all | solution.py:144
  217.4 0.0 copy-start.1
  217.4 0.0 copy-start.2
  217.4 0.2 fusion.56
  217.6 0.8 copy-done.1
  218.5 0.2 copy-done.2
  218.6 2.6 %fusion.18 = f32[512,1024]{1,0:T(8,128)} fusion(bf16[512,1024]{1,0:T(8,128)(2,1)S(1)} %get-tuple-element.8, bf16[512,1024]{1,0:T(8,128)(2,1)S(1)} %get-tuple-element.7, bf16[512,512]{1,0:T(8,128)(2,1)S(1)} %copy-done.2, bf16[512,512]{1,0:T(8,128)(2,1)S(1)} %copy-done.1), kind=kOutput, calls=%fused_computation.24 | convolution fusion | flops 1080033280 | bytes 5242880 | tf_op jit(solution)/shard_map/dot_general | solution.py:150
  (9 shorter events, 0.1 us)
Async XLA Ops:
  0.0 10.7 %copy-start = (bf16[512,1024]{1,0:T(8,128)(2,1)S(1)}, bf16[512,1024]{1,0:T(8,128)(2,1)}, u32[]{:S(2)}) copy-start(bf16[512,1024]{1,0:T(8,128)(2,1)} %param.5) | copy-start | bytes 3145732
  13.9 10.7 %copy-start.7 = (s32[2,32]{1,0:T(2,128)S(1)}, s32[2,32]{1,0:T(2,128)}, u32[]{:S(2)}) copy-start(s32[2,32]{1,0:T(2,128)} %param.8) | copy-start | bytes 772
  13.9 58.7 %all-to-all-start = ((bf16[32,16,2048]{2,1,0:T(8,128)(2,1)}), bf16[32,16,2048]{2,1,0:T(8,128)(2,1)S(1)}, u32[]{:S(2)}, u32[]{:S(2)}) async-start(bf16[32,16,2048]{2,1,0:T(8,128)(2,1)} %pad_maximum_fusion), calls=%async_computation | async-start | bytes 4194304 | tf_op jit(solution)/shard_map/all_to_all | solution.py:18
  72.9 1.0 copy-start.3
  73.0 1.2 copy-start.4
  73.0 1.3 copy-start.5
  74.3 16.3 %copy-start.6 = (s32[2,32]{1,0:T(2,128)S(1)}, s32[2,32]{1,0:T(2,128)}, u32[]{:S(2)}) copy-start(s32[2,32]{1,0:T(2,128)} %param.9) | copy-start | bytes 772
  76.4 32.1 %all-to-all-start.1 = ((bf16[16,2,16,512]{3,2,1,0:T(8,128)(2,1)}), bf16[16,2,16,512]{3,2,1,0:T(8,128)(2,1)S(1)}, u32[]{:S(2)}, u32[]{:S(2)}) async-start(bf16[16,2,16,512]{3,2,1,0:T(8,128)(2,1)} %bitcast.4), calls=%async_computation.1 | async-start | bytes 1048576 | tf_op jit(solution)/shard_map/all_to_all | solution.py:18
  109.4 48.7 %all-to-all-start.2 = ((bf16[16,2,16,512]{3,2,1,0:T(8,128)(2,1)}), bf16[16,2,16,512]{3,2,1,0:T(8,128)(2,1)S(1)}, u32[]{:S(2)}, u32[]{:S(2)}) async-start(bf16[16,2,16,512]{3,2,1,0:T(8,128)(2,1)} %broadcast_in_dim.11), calls=%async_computation.2 | async-start | bytes 1048576 | tf_op jit(solution)/shard_map/all_to_all | solution.py:30
  217.4 1.0 copy-start.1
  217.4 1.2 copy-start.2
